TPU v7x, 32 devices: a whole 2x2x4 slice. The times are simulated.
32 devices in a mesh: kpt: 4 (over y, x), pw: 8 (over z, core).
Axes of the slice: x: 2, y: 2, z: 4, core: 2. Of those that a mesh axis runs over, the one named last changes fastest.
Arguments:
- energies: float32 [16, 512], P('kpt', 'pw'), may hold values from 0.5 to 3
- current: float32 [2, 16, 512], P(None, 'kpt', 'pw'), may hold values from -40 to 40
- previous: float32 [2, 16, 512], P(None, 'kpt', 'pw'), may hold values from -6 to 6
- previous_beta: float32 [2], replicated, may hold values from 0.5 to 2
- pair_left: bfloat16 [16, 512, 4096], P('kpt', None, 'pw'), may hold values from -0.09375 to 0.09375
- pair_right: bfloat16 [16, 512, 4096], P('kpt', None, 'pw'), may hold values from -0.25 to 0.25
- screened: bfloat16 [16, 4096, 4096], P('kpt', 'pw'), may hold values from -0.0234375 to 0.0234375
- momentum_index: int32 [16, 16], replicated, may hold values from 0 to 15, each once within a row
Outputs:
- last_vector: float32 [2, 16, 512], P(None, 'kpt', 'pw')
- prior_vector: float32 [2, 16, 512], P(None, 'kpt', 'pw')
- alpha_terms: float32 [2, 3], replicated
- beta_terms: float32 [2, 3], replicated
Inputs may be any that keep to these rules, and one draw needn't show every extreme that they name: Each row of momentum_index names every index from 0 to 15 once.
All inputs are finite; a program needn't handle non-finite values.
Results may differ from a plain program's by a relative error of at most 0.003.
Values may be sent and summed in bfloat16 or wider, within the bound.
A program may use at most 128 MiB of HBM per device.

v0:
```python
import jax
import jax.numpy as jnp
from jax import lax
from jax.sharding import PartitionSpec as P

STEPS = 3
epsilon = 1e-06


def screened_images(density, screened):
    kpoint_rows = lax.all_gather(density, "kpt", axis=0, tiled=True)
    return jnp.einsum(
        "qsg,kvg->qkvs",
        screened,
        lax.all_gather(kpoint_rows, "pw", axis=2, tiled=True),
        preferred_element_type=jnp.float32,
    )


def on_device(
    energies, current, previous, previous_beta, pair_left, pair_right, screened, momentum_index
):
    kpoint_total = momentum_index.shape[0]
    band_total = pair_left.shape[1]
    entries = kpoint_total * band_total
    qcount = screened.shape[0]
    qpoints = lax.axis_index("kpt") * qcount + jnp.arange(qcount, dtype=jnp.int32)
    selector = (momentum_index[None, :, :] == qpoints[:, None, None]).astype(jnp.float32)
    vector, earlier, levels = (current, previous, energies)
    beta_before = previous_beta
    alpha_list = []
    beta_list = []
    for turn_index in range(STEPS):
        rounded = vector.astype(jnp.bfloat16)
        rounded = lax.all_gather(rounded, "pw", axis=2, tiled=True)
        density = jnp.einsum(
            "kcg,vkc->kvg", pair_right, rounded, preferred_element_type=jnp.float32
        ).astype(jnp.bfloat16)
        images = screened_images(density, screened)
        partial_field = jnp.einsum(
            "qjk,qkvs->jvs",
            selector,
            images,
            precision=lax.Precision.HIGHEST,
            preferred_element_type=jnp.float32,
        )
        potential = lax.psum_scatter(partial_field, "kpt", scatter_dimension=0, tiled=True).astype(
            jnp.bfloat16
        )
        partial_direct = jnp.einsum(
            "kcs,kvs->vkc", pair_left, potential, preferred_element_type=jnp.float32
        )
        direct = lax.psum_scatter(partial_direct, "pw", scatter_dimension=2, tiled=True)
        applied = levels[None] * vector - direct - beta_before[:, None, None] * earlier
        vector_own = vector
        cross_sum, square_sum, vector_sum = lax.psum(
            (
                jnp.sum(vector_own * applied, axis=(1, 2)),
                jnp.sum(applied * applied, axis=(1, 2)),
                jnp.sum(vector_own * vector_own, axis=(1, 2)),
            ),
            ("kpt", "pw"),
        )
        alpha_now = cross_sum / entries
        mean_square = (
            square_sum / entries
            - 2.0 * alpha_now * (cross_sum / entries)
            + alpha_now * alpha_now * (vector_sum / entries)
        )
        beta_now = jnp.sqrt(mean_square + epsilon)
        residual = applied - alpha_now[:, None, None] * vector
        earlier = vector
        vector = residual / beta_now[:, None, None]
        beta_before = beta_now
        alpha_list.append(alpha_now)
        beta_list.append(beta_now)
    return (vector, earlier, jnp.stack(alpha_list, axis=1), jnp.stack(beta_list, axis=1))


def solution(mesh):
    return jax.shard_map(
        on_device,
        mesh=mesh,
        in_specs=(
            P("kpt", "pw"),
            P(None, "kpt", "pw"),
            P(None, "kpt", "pw"),
            P(),
            P("kpt", None, "pw"),
            P("kpt", None, "pw"),
            P("kpt", "pw", None),
            P(),
        ),
        out_specs=(P(None, "kpt", "pw"), P(None, "kpt", "pw"), P(), P()),
        check_vma=False,
    )
```

profile of v0, /device:TPU:10, one launch (start us, length us, event | category | flops | bytes accessed | tf_op | source)
XLA Modules:
  0.0 434.7 jit_solution(2461469843560152316)
XLA Ops:
  7.2 0.0 reduce-scatter.10.cloned.1.call-start
  7.3 0.8 convert_element_type.28
  8.1 0.1 copy.33
  8.2 14.4 %all_gather.27 = bf16[2,4,512]{1,0,2:T(2,128)(2,1)S(1)} all-gather(bf16[2,4,64]{1,0,2:T(2,128)(2,1)S(1)} %copy.33), channel_id=1, replica_groups=mesh['kpt'=4,'pw'=8] {'pw'}, dimensions={2}, use_global_device_ids=true | all-gather | bytes 9216 | tf_op jit(solution)/shard_map/all_gather | solution.py:35
  22.6 0.1 copy.34
  22.8 0.4 convolution_convert_fusion.2
  23.2 8.2 %all_gather.28 = bf16[16,2,512]{2,1,0:T(2,128)(2,1)S(1)} all-gather(bf16[4,2,512]{2,1,0:T(2,128)(2,1)S(1)} %convolution_convert_fusion.2), channel_id=1, replica_groups=mesh['kpt'=4,'pw'=8] {'kpt'}, dimensions={0}, use_global_device_ids=true | all-gather | bytes 40960 | tf_op jit(solution)/shard_map/all_gather | solution.py:11
  31.4 14.3 %all_gather.29 = bf16[16,2,4096]{2,0,1:T(8,128)(2,1)S(1)} all-gather(bf16[16,2,512]{2,0,1:T(8,128)(2,1)S(1)} %copy.35), channel_id=1, replica_groups=mesh['kpt'=4,'pw'=8] {'pw'}, dimensions={2}, use_global_device_ids=true | all-gather | bytes 294912 | tf_op jit(solution)/shard_map/all_gather | solution.py:15
  45.6 10.8 %fusion.6 = f32[4,16,2,512]{3,1,0,2:T(8,128)S(1)} fusion(bf16[4,512,4096]{2,1,0:T(8,128)(2,1)} %param.14, bf16[16,2,4096]{2,0,1:T(8,128)(2,1)S(1)} %all_gather.29), kind=kOutput, calls=%fused_computation.6 | convolution fusion | flops 536870912 | bytes 17301504 | tf_op jit(solution)/shard_map/qsg,kvg->qkvs/dot_general | solution.py:12
  56.5 0.3 convolution_bitcast_fusion.2
  56.8 0.1 copy.36
  56.9 15.0 %all-reduce = bf16[16,2,512]{2,1,0:T(2,128)(2,1)S(1)} all-reduce(f32[16,2,512]{2,1,0:T(2,128)S(1)} %copy.36), channel_id=2, replica_groups=mesh['kpt'=4,'pw'=8] {'kpt'}, use_global_device_ids=true, to_apply=%region_0.0.clone | all-reduce | flops 16384 | bytes 98304
  71.9 0.6 dynamic-slice
  73.2 2.2 convolution_bitcast_fusion.5
  75.5 0.4 copy.56
  75.9 1.2 reshape.29
  77.1 0.0 reduce-scatter.12.cloned.1.call-start
  77.1 28.3 %reduce-scatter.10.cloned.1.call-done = f32[64,8]{1,0:T(8,128)} async-done(((f32[512,8]{1,0:T(8,128)}), f32[64,8]{1,0:T(8,128)}) %reduce-scatter.10.cloned.1.call-update) | async-done | bytes 2064
  105.4 0.9 reshape.30
  106.3 0.1 copy.37
  106.4 0.2 multiply_reduce_fusion.7
  106.6 43.5 %all-reduce.5 = (f32[2]{0:T(128)S(1)}, f32[2]{0:T(128)S(1)}, f32[2]{0:T(128)S(1)}) all-reduce(f32[2]{0:T(128)S(1)} %get-tuple-element.24, f32[2]{0:T(128)S(1)} %get-tuple-element.23, f32[2]{0:T(128)S(1)} %get-tuple-element.22), channel_id=1, replica_groups=mesh['kpt'=4,'pw'=8] {'kpt','pw'}, use_global_device_ids=true, to_apply=%region_7.0 | all-reduce | flops 6 | bytes 48 | tf_op jit(solution)/shard_map/psum | solution.py:56
  150.1 0.1 fusion.37
  150.2 0.1 copy.38
  150.4 12.4 %all_gather.30 = bf16[2,4,512]{1,0,2:T(2,128)(2,1)S(1)} all-gather(bf16[2,4,64]{1,0,2:T(2,128)(2,1)S(1)} %copy.38), channel_id=1, replica_groups=mesh['kpt'=4,'pw'=8] {'pw'}, dimensions={2}, use_global_device_ids=true | all-gather | bytes 9216 | tf_op jit(solution)/shard_map/all_gather | solution.py:35
  162.8 0.1 copy.39
  162.9 0.4 convolution_convert_fusion.1
  163.3 7.2 %all_gather.31 = bf16[16,2,512]{2,1,0:T(2,128)(2,1)S(1)} all-gather(bf16[4,2,512]{2,1,0:T(2,128)(2,1)S(1)} %convolution_convert_fusion.1), channel_id=1, replica_groups=mesh['kpt'=4,'pw'=8] {'kpt'}, dimensions={0}, use_global_device_ids=true | all-gather | bytes 40960 | tf_op jit(solution)/shard_map/all_gather | solution.py:11
  170.5 14.4 %all_gather.32 = bf16[16,2,4096]{2,0,1:T(8,128)(2,1)S(1)} all-gather(bf16[16,2,512]{2,0,1:T(8,128)(2,1)S(1)} %copy.40), channel_id=1, replica_groups=mesh['kpt'=4,'pw'=8] {'pw'}, dimensions={2}, use_global_device_ids=true | all-gather | bytes 294912 | tf_op jit(solution)/shard_map/all_gather | solution.py:15
  184.9 10.8 %fusion.9 = f32[4,16,2,512]{3,1,0,2:T(8,128)S(1)} fusion(bf16[4,512,4096]{2,1,0:T(8,128)(2,1)} %param.14, bf16[16,2,4096]{2,0,1:T(8,128)(2,1)S(1)} %all_gather.32), kind=kOutput, calls=%fused_computation.7 | convolution fusion | flops 536870912 | bytes 17301504 | tf_op jit(solution)/shard_map/qsg,kvg->qkvs/dot_general | solution.py:12
  195.7 0.4 convolution_bitcast_fusion.1
  196.1 0.1 copy.41
  196.2 15.7 %all-reduce.1 = bf16[16,2,512]{2,1,0:T(2,128)(2,1)S(1)} all-reduce(f32[16,2,512]{2,1,0:T(2,128)S(1)} %copy.41), channel_id=4, replica_groups=mesh['kpt'=4,'pw'=8] {'kpt'}, use_global_device_ids=true, to_apply=%region_8.0.clone | all-reduce | flops 16384 | bytes 98304
  211.8 2.2 convolution_bitcast_fusion.4
  214.1 0.4 copy.58
  214.5 1.2 reshape.31
  215.7 0.0 reduce-scatter.14.cloned.1.call-start
  215.8 27.7 %reduce-scatter.12.cloned.1.call-done = f32[64,8]{1,0:T(8,128)} async-done(((f32[512,8]{1,0:T(8,128)}), f32[64,8]{1,0:T(8,128)}) %reduce-scatter.12.cloned.1.call-update) | async-done | bytes 2064
  243.5 0.9 reshape.32
  244.4 0.1 copy.42
  244.5 0.2 multiply_reduce_fusion.4
  244.7 43.5 %all-reduce.4 = (f32[2]{0:T(128)S(1)}, f32[2]{0:T(128)S(1)}, f32[2]{0:T(128)S(1)}) all-reduce(f32[2]{0:T(128)S(1)} %get-tuple-element.21, f32[2]{0:T(128)S(1)} %get-tuple-element.20, f32[2]{0:T(128)S(1)} %get-tuple-element.19), channel_id=1, replica_groups=mesh['kpt'=4,'pw'=8] {'kpt','pw'}, use_global_device_ids=true, to_apply=%region_15.0 | all-reduce | flops 6 | bytes 48 | tf_op jit(solution)/shard_map/psum | solution.py:56
  288.1 0.1 fusion.36
  288.2 0.1 copy.43
  288.3 12.4 %all_gather.33 = bf16[2,4,512]{1,0,2:T(2,128)(2,1)S(1)} all-gather(bf16[2,4,64]{1,0,2:T(2,128)(2,1)S(1)} %copy.43), channel_id=1, replica_groups=mesh['kpt'=4,'pw'=8] {'pw'}, dimensions={2}, use_global_device_ids=true | all-gather | bytes 9216 | tf_op jit(solution)/shard_map/all_gather | solution.py:35
  300.7 0.1 copy.44
  300.9 0.4 convolution_convert_fusion
  301.3 7.3 %all_gather.34 = bf16[16,2,512]{2,1,0:T(2,128)(2,1)S(1)} all-gather(bf16[4,2,512]{2,1,0:T(2,128)(2,1)S(1)} %convolution_convert_fusion), channel_id=1, replica_groups=mesh['kpt'=4,'pw'=8] {'kpt'}, dimensions={0}, use_global_device_ids=true | all-gather | bytes 40960 | tf_op jit(solution)/shard_map/all_gather | solution.py:11
  308.6 14.2 %all_gather.35 = bf16[16,2,4096]{2,0,1:T(8,128)(2,1)S(1)} all-gather(bf16[16,2,512]{2,0,1:T(8,128)(2,1)S(1)} %copy.45), channel_id=1, replica_groups=mesh['kpt'=4,'pw'=8] {'pw'}, dimensions={2}, use_global_device_ids=true | all-gather | bytes 294912 | tf_op jit(solution)/shard_map/all_gather | solution.py:15
  322.8 10.8 %fusion.12 = f32[4,16,2,512]{3,1,0,2:T(8,128)S(1)} fusion(bf16[4,512,4096]{2,1,0:T(8,128)(2,1)} %param.14, bf16[16,2,4096]{2,0,1:T(8,128)(2,1)S(1)} %all_gather.35), kind=kOutput, calls=%fused_computation.8 | convolution fusion | flops 536870912 | bytes 17301504 | tf_op jit(solution)/shard_map/qsg,kvg->qkvs/dot_general | solution.py:12
  333.6 0.4 convolution_bitcast_fusion
  334.0 0.1 copy.46
  334.1 15.6 %all-reduce.2 = bf16[16,2,512]{2,1,0:T(2,128)(2,1)S(1)} all-reduce(f32[16,2,512]{2,1,0:T(2,128)S(1)} %copy.46), channel_id=6, replica_groups=mesh['kpt'=4,'pw'=8] {'kpt'}, use_global_device_ids=true, to_apply=%region_16.0.clone | all-reduce | flops 16384 | bytes 98304
  349.6 2.2 convolution_bitcast_fusion.3
  351.9 0.4 copy.60
  352.3 1.2 reshape.33
  353.5 28.0 %reduce-scatter.14.cloned.1.call-done = f32[64,8]{1,0:T(8,128)} async-done(((f32[512,8]{1,0:T(8,128)}), f32[64,8]{1,0:T(8,128)}) %reduce-scatter.14.cloned.1.call-update) | async-done | bytes 2064
  381.5 0.9 reshape.34
  382.4 0.1 copy.47
  382.5 0.2 multiply_reduce_fusion.1
  382.7 43.5 %all-reduce.3 = (f32[2]{0:T(128)S(1)}, f32[2]{0:T(128)S(1)}, f32[2]{0:T(128)S(1)}) all-reduce(f32[2]{0:T(128)S(1)} %get-tuple-element.18, f32[2]{0:T(128)S(1)} %get-tuple-element.17, f32[2]{0:T(128)S(1)} %get-tuple-element.16), channel_id=1, replica_groups=mesh['kpt'=4,'pw'=8] {'kpt','pw'}, use_global_device_ids=true, to_apply=%region_23.0 | all-reduce | flops 6 | bytes 48 | tf_op jit(solution)/shard_map/psum | solution.py:56
  426.2 0.6 copy.48
  426.9 0.6 copy.49
  427.5 0.7 subtract_divide_fusion
  (28 shorter events, 0.2 us)
Async XLA Ops:
  7.2 15.6 %copy-start = (bf16[4,512,512]{2,1,0:T(8,128)(2,1)S(1)}, bf16[4,512,512]{2,1,0:T(8,128)(2,1)}, u32[]{:S(2)}) copy-start(bf16[4,512,512]{2,1,0:T(8,128)(2,1)} %param.13) | copy-start | bytes 6291460
  7.2 98.2 %reduce-scatter.10.cloned.1.call-start = ((), (), s32[]{:S(2)}) async-start(), calls=%async_computation.3 | async-start | bytes 294912
  45.6 10.8 %copy-start.1 = (s32[16,16]{1,0:T(8,128)S(1)}, s32[16,16]{1,0:T(8,128)}, u32[]{:S(2)}) copy-start(s32[16,16]{1,0:T(8,128)} %param.15) | copy-start | bytes 3076
  45.6 26.3 %copy-start.7 = (u32[32]{0:T(128)S(1)}, u32[32]{0:T(128)}, u32[]{:S(2)}) copy-start(u32[32]{0:T(128)} %constant.29) | copy-start | bytes 388
  73.2 33.2 %copy-start.2 = (f32[2,4,64]{2,1,0:T(4,128)S(1)}, f32[2,4,64]{2,1,0:T(4,128)}, u32[]{:S(2)}) copy-start(f32[2,4,64]{2,1,0:T(4,128)} %param.9) | copy-start | bytes 6148
  73.2 33.2 %copy-start.4 = (f32[4,64]{1,0:T(4,128)S(1)}, f32[4,64]{1,0:T(4,128)}, u32[]{:S(2)}) copy-start(f32[4,64]{1,0:T(4,128)} %param.8) | copy-start | bytes 3076
  73.2 33.2 %copy-start.5 = (f32[2,4,64]{2,1,0:T(4,128)S(1)}, f32[2,4,64]{2,1,0:T(4,128)}, u32[]{:S(2)}) copy-start(f32[2,4,64]{2,1,0:T(4,128)} %param.10) | copy-start | bytes 6148
  73.2 33.2 %copy-start.6 = (f32[2]{0:T(128)S(1)}, f32[2]{0:T(128)}, u32[]{:S(2)}) copy-start(f32[2]{0:T(128)} %param.11) | copy-start | bytes 28
  77.1 166.4 %reduce-scatter.12.cloned.1.call-start = ((), (), s32[]{:S(2)}) async-start(), calls=%async_computation.4 | async-start | bytes 294912
  215.7 165.8 %reduce-scatter.14.cloned.1.call-start = ((), (), s32[]{:S(2)}) async-start(), calls=%async_computation.5 | async-start | bytes 294912
  288.2 139.3 %copy-start.3 = (f32[2,4,64]{2,1,0:T(4,128)}, f32[2,4,64]{2,1,0:T(4,128)S(1)}, u32[]{:S(2)}) copy-start(f32[2,4,64]{2,1,0:T(4,128)S(1)} %get-tuple-element.36) | copy-start | bytes 6148
Sparse Core Ops, SparseCore 0:
  77.2 28.1 reduce-scatter.9
  215.8 27.6 reduce-scatter.11
  353.6 27.8 reduce-scatter.13
where the time goes:
time: 436 us; the launch traced here: 435 us
  blocking collectives  282 us (65%)
  waiting for transfers between devices  84.1 us (19%)
  matrix products  41.3 us (9%)
  between operations  14.7 us (3%)
  local copies, waits for them, and re-layouts  10.7 us (2%)
    psum x3, blocking collectives, on_device(): lax.psum((jnp.sum(vector_own * applied, axis=(1, 2)), jnp.sum(applied * a...  130 us
    unnamed x6, waiting for transfers between devices  84.1 us
    unnamed x3, blocking collectives  46.3 us
    all_gather x3, blocking collectives, screened_images(): lax.all_gather(kpoint_rows, 'pw', axis=2, tiled=True)  42.9 us
    all_gather x3, blocking collectives, on_device(): rounded = lax.all_gather(rounded, 'pw', axis=2, tiled=True)  39.2 us
    dot_general x3, matrix products, screened_images(): jnp.einsum('qsg,kvg->qkvs', screened, lax.all_gather(kpoint_rows, 'pw', a...  32.4 us
    all_gather x3, blocking collectives, screened_images(): kpoint_rows = lax.all_gather(density, 'kpt', axis=0, tiled=True)  22.8 us
    unnamed x28, local copies, waits for them, and re-layouts  9.34 us
  transfers between devices with their start and end apart: 3, of which 3 were waited for; matrix products, arithmetic and copies ran while one was open for 0% of the time, Pallas kernels for 0%

commit v1 on v0

--- a/solution.py
+++ b/solution.py
@@ -1,3 +1,4 @@
+import functools
 import jax
 import jax.numpy as jnp
 from jax import lax
@@ -5,6 +6,15 @@
 
 STEPS = 3
 epsilon = 1e-06
+
+
+def point_cycles(my_tile, peer_axis, axis_tag):
+    for d in (peer_axis, axis_tag):
+        my_tile = lax.psum(my_tile, d)
+    return my_tile
+
+
+cut_frames_in = functools.partial(point_cycles, peer_axis="pw", axis_tag="kpt")
 
 
 def screened_images(density, screened):
@@ -53,13 +63,12 @@
         direct = lax.psum_scatter(partial_direct, "pw", scatter_dimension=2, tiled=True)
         applied = levels[None] * vector - direct - beta_before[:, None, None] * earlier
         vector_own = vector
-        cross_sum, square_sum, vector_sum = lax.psum(
+        cross_sum, square_sum, vector_sum = cut_frames_in(
             (
                 jnp.sum(vector_own * applied, axis=(1, 2)),
                 jnp.sum(applied * applied, axis=(1, 2)),
                 jnp.sum(vector_own * vector_own, axis=(1, 2)),
-            ),
-            ("kpt", "pw"),
+            )
         )
         alpha_now = cross_sum / entries
         mean_square = (

time: 436 us -> 387 us (0.89); the launches traced: 435 us -> 379 us
  blocking collectives: 282 us -> 224 us
    psum x3 -> x6, blocking collectives: 130 us -> 66.2 us  [point_cycles(): my_tile = lax.psum(my_tile, d)]
    all_gather x3, blocking collectives: 39.2 us -> 43.6 us  [on_device(): rounded = lax.all_gather(rounded, 'pw', axis=2, tiled=True)]
where the time goes in v1:
time: 387 us; the launch traced here: 379 us
  blocking collectives  224 us (58%)
  waiting for transfers between devices  86.3 us (22%)
  matrix products  41.3 us (11%)
  between operations  14.7 us (4%)
  local copies, waits for them, and re-layouts  10.7 us (3%)
    unnamed x6, waiting for transfers between devices  86.3 us
    psum x6, blocking collectives, point_cycles(): my_tile = lax.psum(my_tile, d)  66.2 us
    unnamed x3, blocking collectives  45 us
    all_gather x3, blocking collectives, on_device(): rounded = lax.all_gather(rounded, 'pw', axis=2, tiled=True)  43.6 us
    all_gather x3, blocking collectives, screened_images(): lax.all_gather(kpoint_rows, 'pw', axis=2, tiled=True)  42.9 us
    dot_general x3, matrix products, screened_images(): jnp.einsum('qsg,kvg->qkvs', screened, lax.all_gather(kpoint_rows, 'pw', a...  32.4 us
    all_gather x3, blocking collectives, screened_images(): kpoint_rows = lax.all_gather(density, 'kpt', axis=0, tiled=True)  26.3 us
    unnamed x28, local copies, waits for them, and re-layouts  9.35 us
  transfers between devices with their start and end apart: 3, of which 3 were waited for; matrix products, arithmetic and copies ran while one was open for 0% of the time, Pallas kernels for 0%

profile of v1, /device:TPU:10, one launch (start us, length us, event | category | flops | bytes accessed | tf_op | source)
XLA Modules:
  0.0 379.3 jit_solution(11969798153382101777)
XLA Ops:
  7.3 0.8 convert_element_type.28
  8.1 0.1 copy.33
  8.2 14.4 %all_gather.27 = bf16[2,4,512]{1,0,2:T(2,128)(2,1)S(1)} all-gather(bf16[2,4,64]{1,0,2:T(2,128)(2,1)S(1)} %copy.33), channel_id=1, replica_groups=mesh['kpt'=4,'pw'=8] {'pw'}, dimensions={2}, use_global_device_ids=true | all-gather | bytes 9216 | tf_op jit(solution)/shard_map/all_gather | solution.py:45
  22.6 0.2 copy.34
  22.8 0.4 convolution_convert_fusion.2
  23.2 8.2 %all_gather.28 = bf16[16,2,512]{2,1,0:T(2,128)(2,1)S(1)} all-gather(bf16[4,2,512]{2,1,0:T(2,128)(2,1)S(1)} %convolution_convert_fusion.2), channel_id=1, replica_groups=mesh['kpt'=4,'pw'=8] {'kpt'}, dimensions={0}, use_global_device_ids=true | all-gather | bytes 40960 | tf_op jit(solution)/shard_map/all_gather | solution.py:21
  31.4 14.3 %all_gather.29 = bf16[16,2,4096]{2,0,1:T(8,128)(2,1)S(1)} all-gather(bf16[16,2,512]{2,0,1:T(8,128)(2,1)S(1)} %copy.35), channel_id=1, replica_groups=mesh['kpt'=4,'pw'=8] {'pw'}, dimensions={2}, use_global_device_ids=true | all-gather | bytes 294912 | tf_op jit(solution)/shard_map/all_gather | solution.py:25
  45.7 10.8 %fusion.6 = f32[4,16,2,512]{3,1,0,2:T(8,128)S(1)} fusion(bf16[4,512,4096]{2,1,0:T(8,128)(2,1)} %param.14, bf16[16,2,4096]{2,0,1:T(8,128)(2,1)S(1)} %all_gather.29), kind=kOutput, calls=%fused_computation.6 | convolution fusion | flops 536870912 | bytes 17301504 | tf_op jit(solution)/shard_map/qsg,kvg->qkvs/dot_general | solution.py:22
  56.5 0.3 convolution_bitcast_fusion.2
  56.8 0.1 copy.36
  56.9 15.0 %all-reduce = bf16[16,2,512]{2,1,0:T(2,128)(2,1)S(1)} all-reduce(f32[16,2,512]{2,1,0:T(2,128)S(1)} %copy.36), channel_id=2, replica_groups=mesh['kpt'=4,'pw'=8] {'kpt'}, use_global_device_ids=true, to_apply=%region_0.0.clone | all-reduce | flops 16384 | bytes 98304
  71.9 0.6 dynamic-slice
  73.2 2.2 convolution_bitcast_fusion.5
  75.5 0.4 copy.56
  75.9 1.2 reshape.29
  77.1 28.5 %reduce-scatter.10.cloned.1.call-done = f32[64,8]{1,0:T(8,128)} async-done(((f32[512,8]{1,0:T(8,128)}), f32[64,8]{1,0:T(8,128)}) %reduce-scatter.10.cloned.1.call-update) | async-done | bytes 2064
  105.6 0.9 reshape.30
  106.5 0.1 copy.37
  106.6 0.2 multiply_reduce_fusion.7
  106.8 14.0 %all-reduce.5 = (f32[2]{0:T(128)S(1)}, f32[2]{0:T(128)S(1)}, f32[2]{0:T(128)S(1)}) all-reduce(f32[2]{0:T(128)S(1)} %get-tuple-element.24, f32[2]{0:T(128)S(1)} %get-tuple-element.23, f32[2]{0:T(128)S(1)} %get-tuple-element.22), channel_id=1, replica_groups=mesh['kpt'=4,'pw'=8] {'pw'}, use_global_device_ids=true, to_apply=%region_9.0 | all-reduce | flops 6 | bytes 48 | tf_op jit(solution)/shard_map/psum | solution.py:13
  120.8 8.1 %all-reduce.8 = (f32[2]{0:T(128)S(1)}, f32[2]{0:T(128)S(1)}, f32[2]{0:T(128)S(1)}) all-reduce(f32[2]{0:T(128)S(1)} %get-tuple-element.31, f32[2]{0:T(128)S(1)} %get-tuple-element.32, f32[2]{0:T(128)S(1)} %get-tuple-element.33), channel_id=1, replica_groups=mesh['kpt'=4,'pw'=8] {'kpt'}, use_global_device_ids=true, to_apply=%region_10.0 | all-reduce | flops 6 | bytes 48 | tf_op jit(solution)/shard_map/psum | solution.py:13
  128.9 0.1 fusion.37
  129.0 0.1 copy.38
  129.1 14.6 %all_gather.30 = bf16[2,4,512]{1,0,2:T(2,128)(2,1)S(1)} all-gather(bf16[2,4,64]{1,0,2:T(2,128)(2,1)S(1)} %copy.38), channel_id=1, replica_groups=mesh['kpt'=4,'pw'=8] {'pw'}, dimensions={2}, use_global_device_ids=true | all-gather | bytes 9216 | tf_op jit(solution)/shard_map/all_gather | solution.py:45
  143.7 0.2 copy.39
  143.9 0.4 convolution_convert_fusion.1
  144.3 9.0 %all_gather.31 = bf16[16,2,512]{2,1,0:T(2,128)(2,1)S(1)} all-gather(bf16[4,2,512]{2,1,0:T(2,128)(2,1)S(1)} %convolution_convert_fusion.1), channel_id=1, replica_groups=mesh['kpt'=4,'pw'=8] {'kpt'}, dimensions={0}, use_global_device_ids=true | all-gather | bytes 40960 | tf_op jit(solution)/shard_map/all_gather | solution.py:21
  153.3 14.4 %all_gather.32 = bf16[16,2,4096]{2,0,1:T(8,128)(2,1)S(1)} all-gather(bf16[16,2,512]{2,0,1:T(8,128)(2,1)S(1)} %copy.40), channel_id=1, replica_groups=mesh['kpt'=4,'pw'=8] {'pw'}, dimensions={2}, use_global_device_ids=true | all-gather | bytes 294912 | tf_op jit(solution)/shard_map/all_gather | solution.py:25
  167.7 10.8 %fusion.9 = f32[4,16,2,512]{3,1,0,2:T(8,128)S(1)} fusion(bf16[4,512,4096]{2,1,0:T(8,128)(2,1)} %param.14, bf16[16,2,4096]{2,0,1:T(8,128)(2,1)S(1)} %all_gather.32), kind=kOutput, calls=%fused_computation.7 | convolution fusion | flops 536870912 | bytes 17301504 | tf_op jit(solution)/shard_map/qsg,kvg->qkvs/dot_general | solution.py:22
  178.5 0.4 convolution_bitcast_fusion.1
  178.9 0.1 copy.41
  178.9 15.0 %all-reduce.1 = bf16[16,2,512]{2,1,0:T(2,128)(2,1)S(1)} all-reduce(f32[16,2,512]{2,1,0:T(2,128)S(1)} %copy.41), channel_id=4, replica_groups=mesh['kpt'=4,'pw'=8] {'kpt'}, use_global_device_ids=true, to_apply=%region_11.0.clone | all-reduce | flops 16384 | bytes 98304
  193.9 2.2 convolution_bitcast_fusion.4
  196.2 0.4 copy.58
  196.6 1.2 reshape.31
  197.9 28.9 %reduce-scatter.12.cloned.1.call-done = f32[64,8]{1,0:T(8,128)} async-done(((f32[512,8]{1,0:T(8,128)}), f32[64,8]{1,0:T(8,128)}) %reduce-scatter.12.cloned.1.call-update) | async-done | bytes 2064
  226.7 0.9 reshape.32
  227.6 0.1 copy.42
  227.7 0.2 multiply_reduce_fusion.4
  227.9 14.0 %all-reduce.4 = (f32[2]{0:T(128)S(1)}, f32[2]{0:T(128)S(1)}, f32[2]{0:T(128)S(1)}) all-reduce(f32[2]{0:T(128)S(1)} %get-tuple-element.21, f32[2]{0:T(128)S(1)} %get-tuple-element.20, f32[2]{0:T(128)S(1)} %get-tuple-element.19), channel_id=1, replica_groups=mesh['kpt'=4,'pw'=8] {'pw'}, use_global_device_ids=true, to_apply=%region_20.0 | all-reduce | flops 6 | bytes 48 | tf_op jit(solution)/shard_map/psum | solution.py:13
  241.9 8.0 %all-reduce.7 = (f32[2]{0:T(128)S(1)}, f32[2]{0:T(128)S(1)}, f32[2]{0:T(128)S(1)}) all-reduce(f32[2]{0:T(128)S(1)} %get-tuple-element.28, f32[2]{0:T(128)S(1)} %get-tuple-element.29, f32[2]{0:T(128)S(1)} %get-tuple-element.30), channel_id=1, replica_groups=mesh['kpt'=4,'pw'=8] {'kpt'}, use_global_device_ids=true, to_apply=%region_21.0 | all-reduce | flops 6 | bytes 48 | tf_op jit(solution)/shard_map/psum | solution.py:13
  249.9 0.1 fusion.36
  250.0 0.1 copy.43
  250.1 14.6 %all_gather.33 = bf16[2,4,512]{1,0,2:T(2,128)(2,1)S(1)} all-gather(bf16[2,4,64]{1,0,2:T(2,128)(2,1)S(1)} %copy.43), channel_id=1, replica_groups=mesh['kpt'=4,'pw'=8] {'pw'}, dimensions={2}, use_global_device_ids=true | all-gather | bytes 9216 | tf_op jit(solution)/shard_map/all_gather | solution.py:45
  264.7 0.2 copy.44
  264.9 0.4 convolution_convert_fusion
  265.3 9.0 %all_gather.34 = bf16[16,2,512]{2,1,0:T(2,128)(2,1)S(1)} all-gather(bf16[4,2,512]{2,1,0:T(2,128)(2,1)S(1)} %convolution_convert_fusion), channel_id=1, replica_groups=mesh['kpt'=4,'pw'=8] {'kpt'}, dimensions={0}, use_global_device_ids=true | all-gather | bytes 40960 | tf_op jit(solution)/shard_map/all_gather | solution.py:21
  274.3 14.2 %all_gather.35 = bf16[16,2,4096]{2,0,1:T(8,128)(2,1)S(1)} all-gather(bf16[16,2,512]{2,0,1:T(8,128)(2,1)S(1)} %copy.45), channel_id=1, replica_groups=mesh['kpt'=4,'pw'=8] {'pw'}, dimensions={2}, use_global_device_ids=true | all-gather | bytes 294912 | tf_op jit(solution)/shard_map/all_gather | solution.py:25
  288.6 10.8 %fusion.12 = f32[4,16,2,512]{3,1,0,2:T(8,128)S(1)} fusion(bf16[4,512,4096]{2,1,0:T(8,128)(2,1)} %param.14, bf16[16,2,4096]{2,0,1:T(8,128)(2,1)S(1)} %all_gather.35), kind=kOutput, calls=%fused_computation.8 | convolution fusion | flops 536870912 | bytes 17301504 | tf_op jit(solution)/shard_map/qsg,kvg->qkvs/dot_general | solution.py:22
  299.4 0.4 convolution_bitcast_fusion
  299.7 0.1 copy.46
  299.8 15.0 %all-reduce.2 = bf16[16,2,512]{2,1,0:T(2,128)(2,1)S(1)} all-reduce(f32[16,2,512]{2,1,0:T(2,128)S(1)} %copy.46), channel_id=6, replica_groups=mesh['kpt'=4,'pw'=8] {'kpt'}, use_global_device_ids=true, to_apply=%region_22.0.clone | all-reduce | flops 16384 | bytes 98304
  314.8 2.2 convolution_bitcast_fusion.3
  317.0 0.4 copy.60
  317.5 1.2 reshape.33
  318.6 28.9 %reduce-scatter.14.cloned.1.call-done = f32[64,8]{1,0:T(8,128)} async-done(((f32[512,8]{1,0:T(8,128)}), f32[64,8]{1,0:T(8,128)}) %reduce-scatter.14.cloned.1.call-update) | async-done | bytes 2064
  347.6 0.9 reshape.34
  348.4 0.1 copy.47
  348.5 0.2 multiply_reduce_fusion.1
  348.7 14.0 %all-reduce.3 = (f32[2]{0:T(128)S(1)}, f32[2]{0:T(128)S(1)}, f32[2]{0:T(128)S(1)}) all-reduce(f32[2]{0:T(128)S(1)} %get-tuple-element.18, f32[2]{0:T(128)S(1)} %get-tuple-element.17, f32[2]{0:T(128)S(1)} %get-tuple-element.16), channel_id=1, replica_groups=mesh['kpt'=4,'pw'=8] {'pw'}, use_global_device_ids=true, to_apply=%region_31.0 | all-reduce | flops 6 | bytes 48 | tf_op jit(solution)/shard_map/psum | solution.py:13
  362.7 8.0 %all-reduce.6 = (f32[2]{0:T(128)S(1)}, f32[2]{0:T(128)S(1)}, f32[2]{0:T(128)S(1)}) all-reduce(f32[2]{0:T(128)S(1)} %get-tuple-element.25, f32[2]{0:T(128)S(1)} %get-tuple-element.26, f32[2]{0:T(128)S(1)} %get-tuple-element.27), channel_id=1, replica_groups=mesh['kpt'=4,'pw'=8] {'kpt'}, use_global_device_ids=true, to_apply=%region_32.0 | all-reduce | flops 6 | bytes 48 | tf_op jit(solution)/shard_map/psum | solution.py:13
  370.8 0.6 copy.48
  371.4 0.6 copy.49
  372.1 0.7 subtract_divide_fusion
  (31 shorter events, 0.3 us)
Async XLA Ops:
  7.2 15.6 %copy-start = (bf16[4,512,512]{2,1,0:T(8,128)(2,1)S(1)}, bf16[4,512,512]{2,1,0:T(8,128)(2,1)}, u32[]{:S(2)}) copy-start(bf16[4,512,512]{2,1,0:T(8,128)(2,1)} %param.13) | copy-start | bytes 6291460
  7.2 98.5 %reduce-scatter.10.cloned.1.call-start = ((), (), s32[]{:S(2)}) async-start(), calls=%async_computation.3 | async-start | bytes 294912
  45.6 10.8 %copy-start.1 = (s32[16,16]{1,0:T(8,128)S(1)}, s32[16,16]{1,0:T(8,128)}, u32[]{:S(2)}) copy-start(s32[16,16]{1,0:T(8,128)} %param.15) | copy-start | bytes 3076
  45.6 26.3 %copy-start.7 = (u32[32]{0:T(128)S(1)}, u32[32]{0:T(128)}, u32[]{:S(2)}) copy-start(u32[32]{0:T(128)} %constant.29) | copy-start | bytes 388
  73.2 33.4 %copy-start.2 = (f32[2,4,64]{2,1,0:T(4,128)S(1)}, f32[2,4,64]{2,1,0:T(4,128)}, u32[]{:S(2)}) copy-start(f32[2,4,64]{2,1,0:T(4,128)} %param.9) | copy-start | bytes 6148
  73.2 33.4 %copy-start.4 = (f32[4,64]{1,0:T(4,128)S(1)}, f32[4,64]{1,0:T(4,128)}, u32[]{:S(2)}) copy-start(f32[4,64]{1,0:T(4,128)} %param.8) | copy-start | bytes 3076
  73.2 33.4 %copy-start.5 = (f32[2,4,64]{2,1,0:T(4,128)S(1)}, f32[2,4,64]{2,1,0:T(4,128)}, u32[]{:S(2)}) copy-start(f32[2,4,64]{2,1,0:T(4,128)} %param.10) | copy-start | bytes 6148
  73.2 33.4 %copy-start.6 = (f32[2]{0:T(128)S(1)}, f32[2]{0:T(128)}, u32[]{:S(2)}) copy-start(f32[2]{0:T(128)} %param.11) | copy-start | bytes 28
  77.1 149.6 %reduce-scatter.12.cloned.1.call-start = ((), (), s32[]{:S(2)}) async-start(), calls=%async_computation.4 | async-start | bytes 294912
  197.8 149.8 %reduce-scatter.14.cloned.1.call-start = ((), (), s32[]{:S(2)}) async-start(), calls=%async_computation.5 | async-start | bytes 294912
  250.0 122.1 %copy-start.3 = (f32[2,4,64]{2,1,0:T(4,128)}, f32[2,4,64]{2,1,0:T(4,128)S(1)}, u32[]{:S(2)}) copy-start(f32[2,4,64]{2,1,0:T(4,128)S(1)} %get-tuple-element.45) | copy-start | bytes 6148
Sparse Core Ops, SparseCore 0:
  77.2 28.3 reduce-scatter.9
  197.9 28.7 reduce-scatter.11
  318.8 28.7 reduce-scatter.13
